TPU v7x, 128 devices: a whole 4x4x4 slice. The times are simulated.
128 devices in a mesh: lon: 8 (over z, y_hi), lat: 16 (over y_lo, x, core).
Axes of the slice: x: 4, y: 4 (y_hi: 2, y_lo: 2; y = y_hi * 2 + y_lo), z: 4, core: 2. Of those that a mesh axis runs over, the one named last changes fastest.
Arguments:
- fields: float32 [4, 8, 1024, 3600], P(None, None, 'lat', 'lon'), may hold values from -6 to 6
- thickness: float32 [8], replicated, may hold values from 5 to 250
- cutoff: int32 [256], replicated, may hold values from 2 to 1800
- barotropic: float32 [3, 1024, 3600], P(None, 'lat', 'lon'), may hold values from -6 to 6
- land_sea: int32 [1024, 3600], P('lat', 'lon'), may hold values 0 or 1
Outputs:
- filtered_tracers: float32 [2, 8, 1024, 3600], P(None, None, 'lat', 'lon')
- velocity: float32 [2, 8, 1024, 3600], P(None, None, 'lat', 'lon')
- sea_level: float32 [1024, 3600], P('lat', 'lon')
Inputs may be any that keep to these rules, and one draw needn't show every extreme that they name: `cutoff`: each filtered row's highest kept wavenumber.
All inputs are finite; a program needn't handle non-finite values. No bound on the sum of `land_sea` on one device may be relied on, other than what follows from the above.
Results may differ from a plain program's by a relative error of at most 0.0003.
Values sent between devices are 32-bit elements; how exact they have to be, the bound alone decides.
No kernel may reach another device: no remote copies, remote signals or barrier semaphores. Data moves between devices by JAX's collectives and lax.ppermute only.
A program may use at most 128 MiB of HBM per device.

v0:
```python
import functools
import math
import numpy as np
import jax
import jax.numpy as jnp
from jax import lax
from jax.experimental import pallas as pl
from jax.experimental.pallas import tpu as pltpu
from jax.sharding import PartitionSpec as P


WAVE = 0.65
SUB = 20
POLE_ROWS = 128
MIB = 1 << 20
RIM = 21
ROWH = 24
SEG = 225
HALF = SEG // 2
FOLD = 128
MROW = 120


def cplx_add(a, b):
    return (a[0] + b[0], (b[1] if a[1] is None else a[1] if b[1] is None else a[1] + b[1]))


def cplx_sub(a, b):
    if b[1] is None:
        im = a[1]
    elif a[1] is None:
        im = -b[1]
    else:
        im = a[1] - b[1]
    return (a[0] - b[0], im)


def conj(a):
    return (a[0], None if a[1] is None else -a[1])


def turn(a, num, den):
    num %= den
    if num == 0:
        return a
    c, s = math.cos(2 * math.pi * num / den), math.sin(2 * math.pi * num / den)
    re, im = a
    if (4 * num) % den == 0:
        q = 4 * num // den
        if q == 1:
            return (jnp.zeros_like(re) if im is None else -im, re)
        if q == 2:
            return (-re, None if im is None else -im)
        return (jnp.zeros_like(re) if im is None else im, -re)
    if im is None:
        return (re * c, re * s)
    if abs(abs(c) - abs(s)) < 1e-12:
        h = abs(c)
        sc, ss = math.copysign(1.0, c), math.copysign(1.0, s)
        x = re if sc > 0 else -re
        y = im if ss > 0 else -im
        x2 = re if ss > 0 else -re
        y2 = im if sc > 0 else -im
        return ((x - y) * h, (x2 + y2) * h)
    return (re * c - im * s, re * s + im * c)


def real_dft(xs):
    n = len(xs)
    if n == 2:
        return [(xs[0] + xs[1], None), (xs[0] - xs[1], None)]
    even, odd = real_dft(xs[0::2]), real_dft(xs[1::2])
    out = [None] * (n // 2 + 1)
    for r in range(n // 4 + 1):
        o = turn(odd[r], -r, n)
        out[r] = cplx_add(even[r], o)
        if r != n // 2 - r:
            out[n // 2 - r] = conj(cplx_sub(even[r], o))
    return out


def real_idft(ys):
    n = 2 * (len(ys) - 1)
    if n == 2:
        return [ys[0][0] + ys[1][0], ys[0][0] - ys[1][0]]
    even, odd = [], []
    for r in range(n // 4 + 1):
        a, b = ys[r], conj(ys[n // 2 - r])
        if r in (0,):
            a, b = (a[0], None), (b[0], None)
        if r == n // 4:
            even.append((a[0] + a[0], None))
            o = turn((a[0] - a[0], a[1] + a[1]), r, n) if False else None
            odd.append((-(a[1] + a[1]), None))
            continue
        even.append(cplx_add(a, b))
        odd.append(turn(cplx_sub(a, b), r, n))
    e, o = real_idft(even), real_idft(odd)
    out = [None] * n
    out[0::2], out[1::2] = e, o
    return out


def fft_tables():
    at = np.concatenate([np.arange(1, HALF + 1), [0]])
    ang = 2.0 * np.pi * ((at[:, None] * at[None, :]) % SEG) / SEG
    w = np.zeros((2, FOLD, 2 * FOLD), np.float32)
    for half in (0, FOLD):
        w[0, : HALF + 1, half : half + HALF + 1] = np.cos(ang) / 60.0
        w[1, : HALF + 1, half : half + HALF + 1] = np.sin(ang) / 60.0
    tw = np.zeros((HALF, 16), np.float32)
    for r in range(1, 9):
        a = 2.0 * np.pi * r * np.arange(1, HALF + 1) / (16 * SEG)
        tw[:, r - 1] = np.cos(a)
        tw[:, r + 7] = np.sin(a)
    return w, tw


def split(x):
    hi = x.astype(jnp.bfloat16)
    lo = (x - hi.astype(jnp.float32)).astype(jnp.bfloat16)
    return hi, lo


def backward(x):
    rows = 7 - lax.broadcasted_iota(jnp.int32, x.shape, 0)
    return jnp.take_along_axis(x, rows, axis=0)


def whereabouts():
    lat, bands = lax.axis_index("lat"), lax.axis_size("lat")
    edge = POLE_ROWS // ROWS
    return (lat < edge) | (lat >= bands - edge), lax.axis_index("lon")


def filter_kernel(*refs, slots):
    xs = refs[:slots]
    cut_ref, wh_ref, wl_ref, tw_ref = refs[slots : 4 + slots]
    y_hbm, y_ref, e_scr, o_scr, out_sem = refs[-5:]
    polar, lon = whereabouts()
    seats, _, lanes = y_ref.shape
    groups = [pl.ds(0, lanes)]

    def load(d, rows):
        return xs[0][d, rows, :] if slots == 1 else xs[d][rows, :]

    def put(d, where=y_ref):
        to = d if slots == 1 else (lon + d) % seats
        return pltpu.make_async_copy(where.at[d], y_hbm.at[to], out_sem.at[d])

    two = 2 * lanes

    if slots == 1:

        @pl.when(jnp.logical_not(polar))
        def _():
            for d in range(seats):
                put(d, xs[0]).start()
            for d in range(seats):
                put(d, xs[0]).wait()

    @pl.when(polar)
    def _():
        e_scr[HALF:, :] = jnp.zeros((FOLD - HALF, 9 * two), jnp.float32)
        o_scr[HALF:, :] = jnp.zeros((FOLD - HALF, 9 * two), jnp.float32)

        def spots(g, r):
            at = r * two + g * 128
            return pl.ds(at, 128), pl.ds(at + lanes, 128)

        def twiddles(tw, r):
            c = jnp.broadcast_to(tw[:, r - 1 : r], (8, 128))
            s = jnp.broadcast_to(tw[:, r + 7 : r + 8], (8, 128))
            return c, s

        def forward(g):
            first = real_dft([load(s // 2, pl.ds(s % 2 * SEG, 1)) for s in range(16)])
            for r in range(9):
                re_at, im_at = spots(g, r)
                e_scr[HALF : HALF + 1, re_at] = first[r][0]
                if first[r][1] is not None:
                    e_scr[HALF : HALF + 1, im_at] = first[r][1]
            for i in range(HALF // 8):
                rows = pl.ds(8 * i, 8)
                tw = tw_ref[rows, :]
                za = real_dft([load(s // 2, pl.ds(s % 2 * SEG + 8 * i + 1, 8)) for s in range(16)])
                far = [
                    backward(load(s // 2, pl.ds(s % 2 * SEG + SEG - 8 - 8 * i, 8)))
                    for s in range(16)
                ]
                zb = real_dft(far[-1:] + far[:-1])
                re_at, im_at = spots(g, 0)
                e_scr[rows, re_at] = za[0][0] + zb[0][0]
                o_scr[rows, re_at] = za[0][0] - zb[0][0]
                for r in range(1, 9):
                    c, s = twiddles(tw, r)
                    (ar, ai), (br, bi) = za[r], zb[r]
                    if r == 8:
                        ure, uim, vre, vim = ar * c, -(ar * s), br * c, br * s
                    else:
                        ure, uim = ar * c + ai * s, ai * c - ar * s
                        vre, vim = br * c - bi * s, bi * c + br * s
                    re_at, im_at = spots(g, r)
                    e_scr[rows, re_at] = ure + vre
                    o_scr[rows, re_at] = ure - vre
                    e_scr[rows, im_at] = uim + vim
                    o_scr[rows, im_at] = uim - vim

        for g in range(lanes // 128):
            forward(g)
        row = lax.broadcasted_iota(jnp.int32, (MROW, lanes), 0)
        k16 = jnp.where(row < HALF, 16 * (row + 1), 0)
        cut = jnp.broadcast_to(cut_ref[...], (MROW, lanes))

        def product(which, x):
            both = jnp.concatenate(split(x), axis=0)
            f = lambda a: jnp.dot(a, both, preferred_element_type=jnp.float32)
            return (f(wh_ref[which]) + f(wl_ref[which]))[:MROW]

        for r in range(9):
            col = pl.ds(r * two, lanes if r == 0 else two)
            p, q = product(0, e_scr[:, col]), product(1, o_scr[:, col])
            pr, qr = p[:, :lanes], q[:, :lanes]
            near = k16 + r <= cut
            far = (k16 - r <= cut) & (row < HALF)
            if r == 0:
                ere = jnp.where(near, jnp.where(row < HALF, pr + pr, pr), 0.0)
                oim = jnp.where(near, -(qr + qr), 0.0)
                e_scr[0:MROW, col] = ere
                o_scr[0:MROW, col] = oim
                p, q = product(0, e_scr[:, col]), product(1, o_scr[:, col])
                e_scr[0:MROW, col] = p - q
                o_scr[0:MROW, col] = p + q
                continue
            pi, qi = p[:, lanes:], q[:, lanes:]
            xr = jnp.where(near, pr + qi, 0.0)
            xi = jnp.where(near, pi - qr, 0.0)
            yr = jnp.where(far, pr - qi, 0.0)
            yi = jnp.where(far, pi + qr, 0.0)
            e_scr[0:MROW, col] = jnp.concatenate([xr + yr, xi + yi], axis=1)
            o_scr[0:MROW, col] = jnp.concatenate([xr - yr, xi - yi], axis=1)
            p, q = product(0, e_scr[:, col]), product(1, o_scr[:, col])
            pr, qr, pi, qi = p[:, :lanes], q[:, :lanes], p[:, lanes:], q[:, lanes:]
            e_scr[0:MROW, col] = jnp.concatenate([pr - qi, pi + qr], axis=1)
            o_scr[0:MROW, col] = jnp.concatenate([pr + qi, pi - qr], axis=1)

        def inverse(g):
            lane = groups[g]
            ws = []
            for r in range(9):
                re_at, im_at = spots(g, r)
                im = None if r in (0, 8) else e_scr[HALF : HALF + 1, im_at]
                ws.append((e_scr[HALF : HALF + 1, re_at], im))
            ys = real_idft(ws)
            for s in range(16):
                y_ref[s // 2, pl.ds(s % 2 * SEG, 1), lane] = ys[s]
            for i in range(HALF // 8):
                rows = pl.ds(8 * i, 8)
                tw = tw_ref[rows, :]
                re_at, im_at = spots(g, 0)
                wa, wb = [(e_scr[rows, re_at], None)], [(o_scr[rows, re_at], None)]
                for r in range(1, 9):
                    re_at, im_at = spots(g, r)
                    c, s = twiddles(tw, r)
                    ar, ai, br, bi = e_scr[rows, re_at], e_scr[rows, im_at], o_scr[rows, re_at], o_scr[rows, im_at]
                    wa.append((ar * c - ai * s, None if r == 8 else ai * c + ar * s))
                    wb.append((br * c + bi * s, None if r == 8 else bi * c - br * s))
                ya, yb = real_idft(wa), real_idft(wb)
                for s in range(16):
                    y_ref[s // 2, pl.ds(s % 2 * SEG + 8 * i + 1, 8), lane] = ya[s]
                    y_ref[s // 2, pl.ds(s % 2 * SEG + SEG - 8 - 8 * i, 8), lane] = backward(yb[(s + 1) % 16])

        for g in range(lanes // 128):
            inverse(g)
        for d in range(seats):
            put(d).start()
        for d in range(seats):
            put(d).wait()


def filter_call(xs, cut, tables, twist, shape):
    lanes = xs[0].shape[-1]
    seats = shape[0]
    vmem = pl.BlockSpec(memory_space=pltpu.VMEM)
    far = pl.BlockSpec(memory_space=pltpu.HBM)
    dma = pltpu.SemaphoreType.DMA((seats,))
    operands = (*xs, cut, *tables, twist)
    return pl.pallas_call(
        functools.partial(filter_kernel, slots=len(xs)),
        out_shape=pltpu.HBM(shape, jnp.float32),
        in_specs=[vmem] * len(operands),
        out_specs=far,
        scratch_shapes=[
            pltpu.VMEM((seats, 2 * SEG, lanes), jnp.float32),
            pltpu.VMEM((FOLD, 9 * 2 * lanes), jnp.float32),
            pltpu.VMEM((FOLD, 9 * 2 * lanes), jnp.float32),
            dma,
        ],
        name="polar_filter",
        compiler_params=pltpu.CompilerParams(vmem_limit_bytes=20 * MIB),
    )(*operands)


ROWS = 64
COLS = 450
LANES = 512
FAR = 112


def lane_ids(rows):
    return lax.broadcasted_iota(jnp.int32, (rows, 128), 1)


def rim_kernel(flow_ref, land_ref, first_ref, last_ref, scr):
    lane = lane_ids(ROWS)
    first = jnp.zeros((ROWS, 128), jnp.float32)
    last = first
    for a in range(4):
        if a < 3:
            scr[:, 0:COLS] = flow_ref[a]
        else:
            scr[:, 0:COLS] = land_ref[...].astype(jnp.float32)
        mine = (lane >= RIM * a) & (lane < RIM * (a + 1))
        first = jnp.where(mine, pltpu.roll(scr[:, 0:128], RIM * a, 1), first)
        turn_by = (RIM * (a + 1) - (COLS - 384)) % 128
        last = jnp.where(mine, pltpu.roll(scr[:, 384:512], turn_by, 1), last)
    first_ref[...] = first
    last_ref[...] = last


def join_kernel(flow_ref, land_ref, east_ref, west_ref, mid_ref, top_ref, low_ref):
    lane = lane_ids(ROWS)
    for a in range(4):
        if a < 3:
            mid_ref[a, :, 0:COLS] = flow_ref[a]
        else:
            mid_ref[a, :, 0:COLS] = land_ref[...].astype(jnp.float32)
        own = mid_ref[a, :, 384:512]
        west = pltpu.roll(west_ref[...], 128 - RIM * (a + 1), 1)
        east = pltpu.roll(east_ref[...], (COLS - 384 - RIM * a) % 128, 1)
        west = jnp.where(lane >= 128 - RIM, west, 0.0)
        east = jnp.where(lane < COLS - 384 + RIM, east, west)
        mid_ref[a, :, 384:512] = jnp.where(lane < COLS - 384, own, east)
        top_ref[a] = mid_ref[a, 0:ROWH]
        low_ref[a] = mid_ref[a, ROWS - ROWH :]


def step_kernel(at_ref, mid_ref, top_ref, low_ref, out_ref, sea_ref, s_scr, e_scr, n_scr, oc_scr, eo_scr, no_scr):
    first_row = at_ref[0] * ROWS - ROWH
    total = at_ref[1]
    for a, scr in enumerate((s_scr, e_scr, n_scr, oc_scr)):
        scr[0:8] = jnp.zeros((8, LANES), jnp.float32)
        scr[8 + FAR :] = jnp.zeros((8, LANES), jnp.float32)
        scr[8 : 8 + ROWH] = top_ref[a]
        scr[8 + ROWH : 8 + ROWH + ROWS] = mid_ref[a]
        scr[8 + ROWH + ROWS : 8 + FAR] = low_ref[a]
    for b in range(FAR // 8):
        at = 8 + 8 * b
        oc = oc_scr[at : at + 8]
        row = first_row + 8 * b + lax.broadcasted_iota(jnp.int32, (8, LANES), 0)
        last = (row == total - 1) | (row == -1)
        eo = oc * pltpu.roll(oc, LANES - 1, 1)
        no = jnp.where(last, 0.0, oc * oc_scr[at + 1 : at + 9])
        eo_scr[at : at + 8] = eo
        no_scr[at : at + 8] = no
        e_scr[at : at + 8] = e_scr[at : at + 8] * eo
        n_scr[at : at + 8] = n_scr[at : at + 8] * no

    def step(_, carry):
        for b in range(FAR // 8):
            at = 8 + 8 * b
            e = e_scr[at : at + 8]
            div = e - pltpu.roll(e, 1, 1) + n_scr[at : at + 8] - n_scr[at - 1 : at + 7]
            s_scr[at : at + 8] = s_scr[at : at + 8] - WAVE * oc_scr[at : at + 8] * div
        for b in range(FAR // 8):
            at = 8 + 8 * b
            s = s_scr[at : at + 8]
            e_scr[at : at + 8] = eo_scr[at : at + 8] * (
                e_scr[at : at + 8] - WAVE * (pltpu.roll(s, LANES - 1, 1) - s)
            )
            n_scr[at : at + 8] = no_scr[at : at + 8] * (
                n_scr[at : at + 8] - WAVE * (s_scr[at + 1 : at + 9] - s)
            )
        return carry

    lax.fori_loop(0, SUB, step, 0)
    mine = slice(8 + ROWH, 8 + ROWH + ROWS)
    sea_ref[...] = s_scr[mine, 0:COLS]
    for a, scr in enumerate((e_scr, n_scr, eo_scr, no_scr)):
        out_ref[a] = scr[mine, 0:COLS]


def vm():
    return pl.BlockSpec(memory_space=pltpu.VMEM)


def hbm():
    return pl.BlockSpec(memory_space=pltpu.HBM)


def sm():
    return pl.BlockSpec(memory_space=pltpu.SMEM)


def f32(*dims):
    return jax.ShapeDtypeStruct(dims, jnp.float32)


def barotropic_rims(flow, land, shift):
    first, last = pl.pallas_call(
        rim_kernel,
        out_shape=(f32(ROWS, 128), f32(ROWS, 128)),
        in_specs=[vm(), vm()],
        out_specs=(vm(), vm()),
        scratch_shapes=[pltpu.VMEM((ROWS, LANES), jnp.float32)],
        name="rim_columns",
        compiler_params=pltpu.CompilerParams(vmem_limit_bytes=8 * MIB),
    )(flow, land)
    east = shift(first, "lon", -1)
    west = shift(last, "lon", 1)
    return east, west


def barotropic_steps(flow, land, east, west, lat_index, total_rows, shift):
    mid, top, low = pl.pallas_call(
        join_kernel,
        out_shape=(f32(4, ROWS, LANES), f32(4, ROWH, LANES), f32(4, ROWH, LANES)),
        in_specs=[vm()] * 4,
        out_specs=(vm(), vm(), vm()),
        name="join_columns",
        compiler_params=pltpu.CompilerParams(vmem_limit_bytes=8 * MIB),
    )(flow, land, east, west)
    above = shift(low, "lat", 1)
    below = shift(top, "lat", -1)
    where = jnp.stack([lat_index, jnp.int32(total_rows)])
    return pl.pallas_call(
        step_kernel,
        out_shape=(f32(4, ROWS, COLS), f32(ROWS, COLS)),
        in_specs=[sm()] + [vm()] * 3,
        out_specs=(vm(), vm()),
        scratch_shapes=[pltpu.VMEM((FAR + 16, LANES), jnp.float32)] * 6,
        name="subcycles",
        compiler_params=pltpu.CompilerParams(vmem_limit_bytes=8 * MIB),
    )(where, mid, above, below)


def pack_flow_kernel(thick_ref, x_hbm, out_hbm, x_scr, y_scr, in_sem, out_sem):
    parts = out_hbm.shape[0]
    levels = thick_ref.shape[0]
    skip = x_hbm.shape[0] // 2
    per = skip // parts
    gets, puts = [], []
    for p in range(parts):
        span = pl.ds(skip + p * per, per)
        gets.append(pltpu.make_async_copy(x_hbm.at[span], x_scr.at[pl.ds(p * per, per)], in_sem.at[p]))
        gets[-1].start()
    whole = thick_ref[0]
    for k in range(1, levels):
        whole = whole + thick_ref[k]
    scale = 1.0 / jnp.full((1, COLS), whole, jnp.float32)
    group = levels // per
    for p in range(0, parts, group):
        for q in range(group):
            gets[p + q].wait()
        mean = thick_ref[0] * x_scr[p * per]
        for k in range(1, levels):
            mean = mean + thick_ref[k] * x_scr[p * per + k]
        mean = mean * scale
        for q in range(p, p + group):
            y_scr[q] = jnp.concatenate([x_scr[q * per + i] - mean for i in range(per)], axis=0).T
            puts.append(pltpu.make_async_copy(y_scr.at[q], out_hbm.at[q], out_sem.at[q]))
            puts[-1].start()
    for copy in puts:
        copy.wait()


def pack_tracer_kernel(x_hbm, *refs):
    parts = len(refs) - 4
    outs = refs[:parts]
    x_scr, y_scr, in_sem, out_sem = refs[parts:]
    per = x_scr.shape[1]
    polar, lon = whereabouts()

    @pl.when(polar)
    def _():
        gets, puts = [], []
        for k in range(parts):
            span = pl.ds((lon + parts - k) % parts * per, per)
            gets.append(pltpu.make_async_copy(x_hbm.at[span], x_scr.at[k], in_sem.at[k]))
            gets[-1].start()
        for k in range(parts):
            gets[k].wait()
            y_scr[k] = jnp.concatenate([x_scr[k, i] for i in range(per)], axis=0).T
            puts.append(pltpu.make_async_copy(y_scr.at[k], outs[k], out_sem.at[k]))
            puts[-1].start()
        for copy in puts:
            copy.wait()


def unpack_flow_kernel(got_ref, new_ref, speed_hbm, v_scr, v_sem):
    parts = got_ref.shape[0]
    per = speed_hbm.shape[0] // parts
    puts = []
    for p in range(parts):
        field = p // (parts // 2)
        block = got_ref[p].T
        for k in range(per):
            piece = block[k * ROWS : (k + 1) * ROWS]
            v_scr[p, k] = new_ref[2 + field] * (piece + new_ref[field])
        puts.append(pltpu.make_async_copy(v_scr.at[p], speed_hbm.at[pl.ds(p * per, per)], v_sem.at[p]))
        puts[-1].start()
    for copy in puts:
        copy.wait()


def unpack_tracer_kernel(got_hbm, x_hbm, tracer_hbm, got_scr, t_scr, in_sem, out_sem):
    parts = got_hbm.shape[0]
    per = tracer_hbm.shape[0] // parts
    polar, _ = whereabouts()

    def get(p):
        return pltpu.make_async_copy(got_hbm.at[p], got_scr.at[p], in_sem.at[p])

    def keep(p):
        return pltpu.make_async_copy(x_hbm.at[pl.ds(p * per, per)], t_scr.at[p], in_sem.at[p])

    def put(p):
        return pltpu.make_async_copy(t_scr.at[p], tracer_hbm.at[pl.ds(p * per, per)], out_sem.at[p])

    @pl.when(polar)
    def _():
        for p in range(parts):
            get(p).start()
        for p in range(parts):
            get(p).wait()
            block = got_scr[p].T
            for k in range(per):
                t_scr[p, k] = block[k * ROWS : (k + 1) * ROWS]
            put(p).start()

    @pl.when(jnp.logical_not(polar))
    def _():
        for p in range(parts):
            keep(p).start()
        for p in range(parts):
            keep(p).wait()
            put(p).start()

    for p in range(parts):
        put(p).wait()


def shift(value, axis, by):
    size = lax.axis_size(axis)
    return lax.ppermute(value, axis, [(i, (i + by) % size) for i in range(size)])


def body(fields, thickness, cutoff, barotropic, land_sea):
    lon_count = lax.axis_size("lon")
    lat_count = lax.axis_size("lat")
    lat = lax.axis_index("lat")
    components, levels, band_rows, tile_cols = fields.shape
    total_rows = band_rows * lat_count
    pole_rows = cutoff.shape[0] // 2
    pole_bands = pole_rows // band_rows
    bands = [b for b in range(lat_count) if b < pole_bands or b >= lat_count - pole_bands]
    table, twist = fft_tables()
    tables = split(jnp.asarray(table))
    twist = jnp.asarray(twist)
    at = jnp.where(lat < pole_bands, lat * band_rows, lat * band_rows - (total_rows - 2 * pole_rows))
    cuts = lax.dynamic_slice_in_dim(cutoff, jnp.clip(at, 0, 2 * pole_rows - band_rows), band_rows)
    pairs = components * levels
    per = pairs // 2 // lon_count
    half = per * band_rows
    cuts = jnp.tile(cuts, per)[None, :]
    dma = pltpu.SemaphoreType.DMA((lon_count,))
    seats = range(lon_count)
    rows_in = fields.reshape(pairs, band_rows, tile_cols)
    parts = pl.pallas_call(
        pack_flow_kernel,
        out_shape=pltpu.HBM((lon_count, tile_cols, half), jnp.float32),
        in_specs=[sm(), hbm()],
        out_specs=hbm(),
        scratch_shapes=[
            pltpu.VMEM((pairs // 2, band_rows, tile_cols), jnp.float32),
            pltpu.VMEM((lon_count, tile_cols, half), jnp.float32),
            dma,
            dma,
        ],
        name="pack_flow",
        compiler_params=pltpu.CompilerParams(vmem_limit_bytes=60 * MIB),
    )(thickness, rows_in)
    parts = lax.all_to_all(parts, "lon", split_axis=0, concat_axis=0)
    slots = pl.pallas_call(
        pack_tracer_kernel,
        out_shape=[pltpu.HBM((tile_cols, half), jnp.float32) for _ in seats],
        in_specs=[hbm()],
        out_specs=[hbm() for _ in seats],
        scratch_shapes=[
            pltpu.VMEM((lon_count, per, band_rows, tile_cols), jnp.float32),
            pltpu.VMEM((lon_count, tile_cols, half), jnp.float32),
            dma,
            dma,
        ],
        name="pack_tracers",
        compiler_params=pltpu.CompilerParams(vmem_limit_bytes=60 * MIB),
    )(rows_in)
    got = [slots[0]]
    for k in range(1, lon_count):
        route = [
            (i * lat_count + b, (i + lon_count - k) % lon_count * lat_count + b) for b in bands for i in seats
        ]
        got.append(lax.ppermute(slots[k], ("lon", "lat"), route))
    shape = (lon_count, tile_cols, half)
    parts = filter_call([parts], cuts, tables, twist, shape)
    parts = lax.all_to_all(parts, "lon", split_axis=0, concat_axis=0)
    east, west = barotropic_rims(barotropic, land_sea, shift)
    got = filter_call(got, cuts, tables, twist, shape)
    got = lax.all_to_all(got, "lon", split_axis=0, concat_axis=0)
    new, sea_level = barotropic_steps(barotropic, land_sea, east, west, lat, total_rows, shift)
    out = pltpu.HBM((pairs // 2, band_rows, tile_cols), jnp.float32)
    rows_scr = pltpu.VMEM((lon_count, per, band_rows, tile_cols), jnp.float32)
    velocity = pl.pallas_call(
        unpack_flow_kernel,
        out_shape=out,
        in_specs=[vm(), vm()],
        out_specs=hbm(),
        scratch_shapes=[rows_scr, dma],
        name="unpack_flow",
        compiler_params=pltpu.CompilerParams(vmem_limit_bytes=16 * MIB),
    )(parts, new)
    tracers = pl.pallas_call(
        unpack_tracer_kernel,
        out_shape=out,
        in_specs=[hbm(), hbm()],
        out_specs=hbm(),
        scratch_shapes=[pltpu.VMEM(shape, jnp.float32), rows_scr, dma, dma],
        name="unpack_tracers",
        compiler_params=pltpu.CompilerParams(vmem_limit_bytes=58 * MIB),
    )(got, rows_in)
    back = (2, levels, band_rows, tile_cols)
    return (tracers.reshape(back), velocity.reshape(back), sea_level)


def solution(mesh):
    return jax.shard_map(
        body,
        mesh=mesh,
        in_specs=(P(None, None, "lat", "lon"), P(), P(), P(None, "lat", "lon"), P("lat", "lon")),
        out_specs=(P(None, None, "lat", "lon"), P(None, None, "lat", "lon"), P("lat", "lon")),
        check_vma=False,
    )
```

profile of v0, /device:TPU:0, one launch (start us, length us, event | category | flops | bytes accessed | tf_op | source)
XLA Modules:
  0.0 149.3 jit_solution(10059696388826210529)
XLA Ops:
  0.6 3.5 %pack_flow.1 = f32[8,450,128]{2,1,0:T(8,128)} custom-call(f32[8]{0:T(128)} %thick_ref.1, f32[32,64,450]{2,1,0:T(8,128)} %bitcast.4), custom_call_target="tpu_custom_call" | custom-call | tf_op jit(solution)/shard_map/pack_flow/pallas_call | solution.py:579
  4.1 8.1 %all-to-all-start.1 = ((f32[8,450,128]{2,1,0:T(8,128)}), f32[8,450,128]{2,1,0:T(8,128)S(1)}, u32[]{:S(2)}, u32[]{:S(2)}) async-start(f32[8,450,128]{2,1,0:T(8,128)} %pack_flow.1), calls=%async_computation.1 | async-start | bytes 3735552 | tf_op jit(solution)/shard_map/all_to_all | solution.py:593
  12.2 2.9 %pack_tracers.1 = (f32[450,128]{1,0:T(8,128)}, f32[450,128]{1,0:T(8,128)}, f32[450,128]{1,0:T(8,128)}, f32[450,128]{1,0:T(8,128)}, f32[450,128]{1,0:T(8,128)}, /...) custom-call(f32[32,64,450]{2,1,0:T(8,128)} %bitcast.5), custom_call_target="tpu_custom_call" | custom-call | tf_op jit(solution)/shard_map/pack_tracers/pallas_call | solution.py:594
  15.2 7.5 %collective-permute-start = (f32[450,128]{1,0:T(8,128)}, f32[450,128]{1,0:T(8,128)S(1)}, u32[]{:S(2)}, u32[]{:S(2)}) collective-permute-start(f32[450,128]{1,0:T(8,128)} %get-tuple-element.19), channel_id=1, source_target_pairs={{0,112},{16,0},{32,16},{48,32},{64,48},{80,64},{96,80},{112,96},{1... | collective-permute-start | bytes 691208 | tf_op jit(solution)/shard_map/ppermute | solution.py:613
  22.7 2.8 %collective-permute-start.1 = (f32[450,128]{1,0:T(8,128)}, f32[450,128]{1,0:T(8,128)S(1)}, u32[]{:S(2)}, u32[]{:S(2)}) collective-permute-start(f32[450,128]{1,0:T(8,128)} %get-tuple-element.20), channel_id=1, source_target_pairs={{0,96},{16,112},{32,0},{48,16},{64,32},{80,48},{96,64},{112,80},{1... | collective-permute-start | bytes 691208 | tf_op jit(solution)/shard_map/ppermute | solution.py:613
  25.5 2.5 %collective-permute-start.2 = (f32[450,128]{1,0:T(8,128)}, f32[450,128]{1,0:T(8,128)S(1)}, u32[]{:S(2)}, u32[]{:S(2)}) collective-permute-start(f32[450,128]{1,0:T(8,128)} %get-tuple-element.21), channel_id=1, source_target_pairs={{0,80},{16,96},{32,112},{48,0},{64,16},{80,32},{96,48},{112,64},{1... | collective-permute-start | bytes 691208 | tf_op jit(solution)/shard_map/ppermute | solution.py:613
  27.9 4.6 %collective-permute-start.3 = (f32[450,128]{1,0:T(8,128)}, f32[450,128]{1,0:T(8,128)S(1)}, u32[]{:S(2)}, u32[]{:S(2)}) collective-permute-start(f32[450,128]{1,0:T(8,128)} %get-tuple-element.22), channel_id=1, source_target_pairs={{0,64},{16,80},{32,96},{48,112},{64,0},{80,16},{96,32},{112,48},{1... | collective-permute-start | bytes 691208 | tf_op jit(solution)/shard_map/ppermute | solution.py:613
  32.5 3.1 %collective-permute-start.4 = (f32[450,128]{1,0:T(8,128)}, f32[450,128]{1,0:T(8,128)S(1)}, u32[]{:S(2)}, u32[]{:S(2)}) collective-permute-start(f32[450,128]{1,0:T(8,128)} %get-tuple-element.23), channel_id=1, source_target_pairs={{0,48},{16,64},{32,80},{48,96},{64,112},{80,0},{96,16},{112,32},{1... | collective-permute-start | bytes 691208 | tf_op jit(solution)/shard_map/ppermute | solution.py:613
  35.7 7.4 %collective-permute-done.refs_1_ = f32[450,128]{1,0:T(8,128)S(1)} collective-permute-done((f32[450,128]{1,0:T(8,128)}, f32[450,128]{1,0:T(8,128)S(1)}, u32[]{:S(2)}, u32[]{:S(2)}) %collective-permute-start) | collective-permute-done | bytes 230432 | tf_op jit(solution)/shard_map/ppermute | solution.py:613
  43.1 2.8 %collective-permute-start.5 = (f32[450,128]{1,0:T(8,128)}, f32[450,128]{1,0:T(8,128)S(1)}, u32[]{:S(2)}, u32[]{:S(2)}) collective-permute-start(f32[450,128]{1,0:T(8,128)} %get-tuple-element.24), channel_id=1, source_target_pairs={{0,32},{16,48},{32,64},{48,80},{64,96},{80,112},{96,0},{112,16},{1... | collective-permute-start | bytes 691208 | tf_op jit(solution)/shard_map/ppermute | solution.py:613
  45.9 8.6 %collective-permute-start.6 = (f32[450,128]{1,0:T(8,128)}, f32[450,128]{1,0:T(8,128)}, u32[]{:S(2)}, u32[]{:S(2)}) collective-permute-start(f32[450,128]{1,0:T(8,128)} %get-tuple-element.25), channel_id=1, source_target_pairs={{0,16},{16,32},{32,48},{48,64},{64,80},{80,96},{96,112},{112,0},{1... | collective-permute-start | bytes 691208 | tf_op jit(solution)/shard_map/ppermute | solution.py:613
  54.7 6.5 %collective-permute-done.5.refs_6_ = f32[450,128]{1,0:T(8,128)S(1)} collective-permute-done((f32[450,128]{1,0:T(8,128)}, f32[450,128]{1,0:T(8,128)S(1)}, u32[]{:S(2)}, u32[]{:S(2)}) %collective-permute-start.5) | collective-permute-done | bytes 230432 | tf_op jit(solution)/shard_map/ppermute | solution.py:613
  63.0 6.0 %polar_filter.2 = f32[8,450,128]{2,1,0:T(8,128)} custom-call(f32[450,128]{1,0:T(8,128)S(1)} %copy-done.4, f32[450,128]{1,0:T(8,128)S(1)} %collective-permute-done.refs_1_, f32[450,128]{1,0:T(8,128)S(1)} %collective-permute-done.1.refs_2_, f32[450,128]{1,0:T(8,128)S(1)} %collective-permute-done.2.refs_3_, f32[450,128]{1,0:T(8,128)S(1)} %collective-permute-done.3.refs_4_, ...), custom_call_target="tpu_custom_call" | custom-call | tf_op jit(solution)/shard_map/polar_filter/pallas_call | solution.py:288
  69.0 6.0 %all-to-all-start = ((f32[8,450,128]{2,1,0:T(8,128)}), f32[8,450,128]{2,1,0:T(8,128)}, u32[]{:S(2)}, u32[]{:S(2)}) async-start(f32[8,450,128]{2,1,0:T(8,128)} %polar_filter.2), calls=%async_computation | async-start | bytes 3735552 | tf_op jit(solution)/shard_map/all_to_all | solution.py:619
  75.0 5.0 %polar_filter.3 = f32[8,450,128]{2,1,0:T(8,128)} custom-call(f32[8,450,128]{2,1,0:T(8,128)S(1)} %all-to-all-done.1.refs_0_, s32[1,128]{1,0:T(1,128)S(1)} %broadcast_in_dim_tile.3.refs_8_.refs_1_, bf16[2,128,256]{2,1,0:T(8,128)(2,1)S(1)} %copy-done.2, bf16[2,128,256]{2,1,0:T(8,128)(2,1)S(1)} %copy-done.1, f32[112,16]{1,0:T(8,128)S(1)} %copy-done.6), custom_call_target="tpu_custom_call" | custom-call | tf_op jit(solution)/shard_map/polar_filter/pallas_call | solution.py:288
  80.0 20.4 %all-to-all-done.got_hbm = f32[8,450,128]{2,1,0:T(8,128)} async-done(((f32[8,450,128]{2,1,0:T(8,128)}), f32[8,450,128]{2,1,0:T(8,128)}, u32[]{:S(2)}, u32[]{:S(2)}) %all-to-all-start) | async-done | bytes 1843232 | tf_op jit(solution)/shard_map/all_to_all | solution.py:619
  100.4 3.6 %all-to-all-start.2 = ((f32[8,450,128]{2,1,0:T(8,128)}), f32[8,450,128]{2,1,0:T(8,128)S(1)}, u32[]{:S(2)}, u32[]{:S(2)}) async-start(f32[8,450,128]{2,1,0:T(8,128)} %polar_filter.3), calls=%async_computation.2 | async-start | bytes 3735552 | tf_op jit(solution)/shard_map/all_to_all | solution.py:616
  104.2 5.6 %collective-permute-start.7 = (f32[64,128]{1,0:T(8,128)S(1)}, f32[64,128]{1,0:T(8,128)S(1)}, u32[]{:S(2)}, u32[]{:S(2)}) collective-permute-start(f32[64,128]{1,0:T(8,128)S(1)} %get-tuple-element.26), channel_id=1, source_target_pairs={{0,112},{16,0},{32,16},{48,32},{64,48},{80,64},{96,80},{112,96},{1... | collective-permute-start | bytes 98312 | tf_op jit(solution)/shard_map/ppermute | solution.py:555
  109.8 18.4 %collective-permute-done.7.east_ref = f32[64,128]{1,0:T(8,128)S(1)} collective-permute-done((f32[64,128]{1,0:T(8,128)S(1)}, f32[64,128]{1,0:T(8,128)S(1)}, u32[]{:S(2)}, u32[]{:S(2)}) %collective-permute-start.7) | collective-permute-done | bytes 32800 | tf_op jit(solution)/shard_map/ppermute | solution.py:555
  128.2 2.5 %collective-permute-done.8.west_ref = f32[64,128]{1,0:T(8,128)S(1)} collective-permute-done((f32[64,128]{1,0:T(8,128)S(1)}, f32[64,128]{1,0:T(8,128)S(1)}, u32[]{:S(2)}, u32[]{:S(2)}) %collective-permute-start.8) | collective-permute-done | bytes 32800 | tf_op jit(solution)/shard_map/ppermute | solution.py:555
  130.9 3.8 %collective-permute-start.10 = (f32[4,24,512]{2,1,0:T(8,128)S(1)}, f32[4,24,512]{2,1,0:T(8,128)S(1)}, u32[]{:S(2)}, u32[]{:S(2)}) collective-permute-start(f32[4,24,512]{2,1,0:T(8,128)S(1)} %get-tuple-element.30), channel_id=1, source_target_pairs={{0,15},{1,0},{2,1},{3,2},{4,3},{5,4},{6,5},{7,6},{8,7},{9,8},{10,9... | collective-permute-start | bytes 589832 | tf_op jit(solution)/shard_map/ppermute | solution.py:555
  134.8 3.3 %collective-permute-done.9.top_ref = f32[4,24,512]{2,1,0:T(8,128)S(1)} collective-permute-done((f32[4,24,512]{2,1,0:T(8,128)S(1)}, f32[4,24,512]{2,1,0:T(8,128)S(1)}, u32[]{:S(2)}, u32[]{:S(2)}) %collective-permute-start.9) | collective-permute-done | bytes 196640 | tf_op jit(solution)/shard_map/ppermute | solution.py:555
  138.1 6.7 %subcycles.1 = (f32[4,64,450]{2,1,0:T(8,128)S(1)}, f32[64,450]{1,0:T(8,128)}) custom-call(s32[2]{0:T(128)S(1)} %pad_add_fusion.at_ref, f32[4,64,512]{2,1,0:T(8,128)S(1)} %get-tuple-element.28.mid_ref, f32[4,24,512]{2,1,0:T(8,128)S(1)} %collective-permute-done.9.top_ref, f32[4,24,512]{2,1,0:T(8,128)S(1)} %collective-permute-done.10.low_ref), custom_call_target="tpu_custom_call" | custom-call | tf_op jit(solution)/shard_map/subcycles/pallas_call | solution.py:436
  144.9 2.9 %unpack_tracers.1 = f32[16,64,450]{2,1,0:T(8,128)} custom-call(f32[8,450,128]{2,1,0:T(8,128)} %all-to-all-done.got_hbm, f32[32,64,450]{2,1,0:T(8,128)} %bitcast.6), custom_call_target="tpu_custom_call" | custom-call | tf_op jit(solution)/shard_map/unpack_tracers/pallas_call | solution.py:632
  (33 shorter events, 3.9 us)
Async XLA Ops:
  4.1 64.9 %all-to-all-start.1 = ((f32[8,450,128]{2,1,0:T(8,128)}), f32[8,450,128]{2,1,0:T(8,128)S(1)}, u32[]{:S(2)}, u32[]{:S(2)}) async-start(f32[8,450,128]{2,1,0:T(8,128)} %pack_flow.1), calls=%async_computation.1 | async-start | bytes 3735552 | tf_op jit(solution)/shard_map/all_to_all | solution.py:593
  12.2 42.4 %copy-start.7 = (s32[256]{0:T(256)S(1)}, s32[256]{0:T(256)}, u32[]{:S(2)}) copy-start(s32[256]{0:T(256)} %param.9) | copy-start | bytes 3076
  12.2 49.1 %copy-start.1 = (bf16[2,128,256]{2,1,0:T(8,128)(2,1)S(1)}, bf16[2,128,256]{2,1,0:T(8,128)(2,1)}, u32[]{:S(2)}) copy-start(bf16[2,128,256]{2,1,0:T(8,128)(2,1)} %constant.31.refs_10_.refs_3_) | copy-start | bytes 393220
  12.2 49.0 %copy-start.2 = (bf16[2,128,256]{2,1,0:T(8,128)(2,1)S(1)}, bf16[2,128,256]{2,1,0:T(8,128)(2,1)}, u32[]{:S(2)}) copy-start(bf16[2,128,256]{2,1,0:T(8,128)(2,1)} %constant.28.refs_9_.refs_2_) | copy-start | bytes 393220
  15.2 27.9 %collective-permute-start = (f32[450,128]{1,0:T(8,128)}, f32[450,128]{1,0:T(8,128)S(1)}, u32[]{:S(2)}, u32[]{:S(2)}) collective-permute-start(f32[450,128]{1,0:T(8,128)} %get-tuple-element.19), channel_id=1, source_target_pairs={{0,112},{16,0},{32,16},{48,32},{64,48},{80,64},{96,80},{112,96},{1... | collective-permute-start | bytes 691208 | tf_op jit(solution)/shard_map/ppermute | solution.py:613
  22.7 23.2 %collective-permute-start.1 = (f32[450,128]{1,0:T(8,128)}, f32[450,128]{1,0:T(8,128)S(1)}, u32[]{:S(2)}, u32[]{:S(2)}) collective-permute-start(f32[450,128]{1,0:T(8,128)} %get-tuple-element.20), channel_id=1, source_target_pairs={{0,96},{16,112},{32,0},{48,16},{64,32},{80,48},{96,64},{112,80},{1... | collective-permute-start | bytes 691208 | tf_op jit(solution)/shard_map/ppermute | solution.py:613
  25.5 29.3 %collective-permute-start.2 = (f32[450,128]{1,0:T(8,128)}, f32[450,128]{1,0:T(8,128)S(1)}, u32[]{:S(2)}, u32[]{:S(2)}) collective-permute-start(f32[450,128]{1,0:T(8,128)} %get-tuple-element.21), channel_id=1, source_target_pairs={{0,80},{16,96},{32,112},{48,0},{64,16},{80,32},{96,48},{112,64},{1... | collective-permute-start | bytes 691208 | tf_op jit(solution)/shard_map/ppermute | solution.py:613
  27.9 26.8 %collective-permute-start.3 = (f32[450,128]{1,0:T(8,128)}, f32[450,128]{1,0:T(8,128)S(1)}, u32[]{:S(2)}, u32[]{:S(2)}) collective-permute-start(f32[450,128]{1,0:T(8,128)} %get-tuple-element.22), channel_id=1, source_target_pairs={{0,64},{16,80},{32,96},{48,112},{64,0},{80,16},{96,32},{112,48},{1... | collective-permute-start | bytes 691208 | tf_op jit(solution)/shard_map/ppermute | solution.py:613
  32.5 22.2 %collective-permute-start.4 = (f32[450,128]{1,0:T(8,128)}, f32[450,128]{1,0:T(8,128)S(1)}, u32[]{:S(2)}, u32[]{:S(2)}) collective-permute-start(f32[450,128]{1,0:T(8,128)} %get-tuple-element.23), channel_id=1, source_target_pairs={{0,48},{16,64},{32,80},{48,96},{64,112},{80,0},{96,16},{112,32},{1... | collective-permute-start | bytes 691208 | tf_op jit(solution)/shard_map/ppermute | solution.py:613
  43.1 18.2 %collective-permute-start.5 = (f32[450,128]{1,0:T(8,128)}, f32[450,128]{1,0:T(8,128)S(1)}, u32[]{:S(2)}, u32[]{:S(2)}) collective-permute-start(f32[450,128]{1,0:T(8,128)} %get-tuple-element.24), channel_id=1, source_target_pairs={{0,32},{16,48},{32,64},{48,80},{64,96},{80,112},{96,0},{112,16},{1... | collective-permute-start | bytes 691208 | tf_op jit(solution)/shard_map/ppermute | solution.py:613
  45.9 15.4 %collective-permute-start.6 = (f32[450,128]{1,0:T(8,128)}, f32[450,128]{1,0:T(8,128)}, u32[]{:S(2)}, u32[]{:S(2)}) collective-permute-start(f32[450,128]{1,0:T(8,128)} %get-tuple-element.25), channel_id=1, source_target_pairs={{0,16},{16,32},{32,48},{48,64},{64,80},{80,96},{96,112},{112,0},{1... | collective-permute-start | bytes 691208 | tf_op jit(solution)/shard_map/ppermute | solution.py:613
  61.3 0.9 copy-start.4
  62.2 0.8 copy-start.5
  69.0 6.0 %copy-start.6 = (f32[112,16]{1,0:T(8,128)S(1)}, f32[112,16]{1,0:T(8,128)}, u32[]{:S(2)}) copy-start(f32[112,16]{1,0:T(8,128)} %constant.24.clone.refs_11_.refs_4_) | copy-start | bytes 21508
  69.0 31.4 %all-to-all-start = ((f32[8,450,128]{2,1,0:T(8,128)}), f32[8,450,128]{2,1,0:T(8,128)}, u32[]{:S(2)}, u32[]{:S(2)}) async-start(f32[8,450,128]{2,1,0:T(8,128)} %polar_filter.2), calls=%async_computation | async-start | bytes 3735552 | tf_op jit(solution)/shard_map/all_to_all | solution.py:619
  80.0 24.0 %copy-start = (f32[3,64,450]{2,1,0:T(8,128)S(1)}, f32[3,64,450]{2,1,0:T(8,128)}, u32[]{:S(2)}) copy-start(f32[3,64,450]{2,1,0:T(8,128)} %flow_ref.3) | copy-start | bytes 1036804
  80.0 24.0 %copy-start.3 = (s32[64,450]{1,0:T(8,128)S(1)}, s32[64,450]{1,0:T(8,128)}, u32[]{:S(2)}) copy-start(s32[64,450]{1,0:T(8,128)} %land_ref.3) | copy-start | bytes 345604
  100.4 47.3 %all-to-all-start.2 = ((f32[8,450,128]{2,1,0:T(8,128)}), f32[8,450,128]{2,1,0:T(8,128)S(1)}, u32[]{:S(2)}, u32[]{:S(2)}) async-start(f32[8,450,128]{2,1,0:T(8,128)} %polar_filter.3), calls=%async_computation.2 | async-start | bytes 3735552 | tf_op jit(solution)/shard_map/all_to_all | solution.py:616
  104.2 24.0 %collective-permute-start.7 = (f32[64,128]{1,0:T(8,128)S(1)}, f32[64,128]{1,0:T(8,128)S(1)}, u32[]{:S(2)}, u32[]{:S(2)}) collective-permute-start(f32[64,128]{1,0:T(8,128)S(1)} %get-tuple-element.26), channel_id=1, source_target_pairs={{0,112},{16,0},{32,16},{48,32},{64,48},{80,64},{96,80},{112,96},{1... | collective-permute-start | bytes 98312 | tf_op jit(solution)/shard_map/ppermute | solution.py:555
  109.8 20.9 %collective-permute-start.8 = (f32[64,128]{1,0:T(8,128)S(1)}, f32[64,128]{1,0:T(8,128)S(1)}, u32[]{:S(2)}, u32[]{:S(2)}) collective-permute-start(f32[64,128]{1,0:T(8,128)S(1)} %get-tuple-element.27), channel_id=1, source_target_pairs={{0,16},{16,32},{32,48},{48,64},{64,80},{80,96},{96,112},{112,0},{1... | collective-permute-start | bytes 98312 | tf_op jit(solution)/shard_map/ppermute | solution.py:555
  130.8 7.3 %collective-permute-start.9 = (f32[4,24,512]{2,1,0:T(8,128)S(1)}, f32[4,24,512]{2,1,0:T(8,128)S(1)}, u32[]{:S(2)}, u32[]{:S(2)}) collective-permute-start(f32[4,24,512]{2,1,0:T(8,128)S(1)} %get-tuple-element.29), channel_id=1, source_target_pairs={{0,1},{1,2},{2,3},{3,4},{4,5},{5,6},{6,7},{7,8},{8,9},{9,10},{10,1... | collective-permute-start | bytes 589832 | tf_op jit(solution)/shard_map/ppermute | solution.py:555
  130.9 7.2 %collective-permute-start.10 = (f32[4,24,512]{2,1,0:T(8,128)S(1)}, f32[4,24,512]{2,1,0:T(8,128)S(1)}, u32[]{:S(2)}, u32[]{:S(2)}) collective-permute-start(f32[4,24,512]{2,1,0:T(8,128)S(1)} %get-tuple-element.30), channel_id=1, source_target_pairs={{0,15},{1,0},{2,1},{3,2},{4,3},{5,4},{6,5},{7,6},{8,7},{9,8},{10,9... | collective-permute-start | bytes 589832 | tf_op jit(solution)/shard_map/ppermute | solution.py:555
where the time goes:
time: 151 us; the launch traced here: 149 us
  starting transfers between devices  59.1 us (39%)
  waiting for transfers between devices  58.5 us (39%)
  Pallas kernels  28.8 us (19%)
  local copies, waits for them, and re-layouts  1.96 us (1%)
    ppermute x7, starting transfers between devices, body(): got.append(lax.ppermute(slots[k], ('lon', 'lat'), route))  31.9 us
    ppermute x4, waiting for transfers between devices, shift(): lax.ppermute(value, axis, [(i, (i + by) % size) for i in range(size)])  24.2 us
    all_to_all x1, waiting for transfers between devices, body(): got = lax.all_to_all(got, 'lon', split_axis=0, concat_axis=0)  20.4 us
    ppermute x7, waiting for transfers between devices, body(): got.append(lax.ppermute(slots[k], ('lon', 'lat'), route))  14 us
    all_to_all x2, starting transfers between devices, body(): parts = lax.all_to_all(parts, 'lon', split_axis=0, concat_axis=0)  11.7 us
    pallas_call x2, Pallas kernels, filter_call(): pl.pallas_call(functools.partial(filter_kernel, slots=len(xs)), out_shape...  10.9 us
    ppermute x4, starting transfers between devices, shift(): lax.ppermute(value, axis, [(i, (i + by) % size) for i in range(size)])  9.55 us
    pallas_call x1, Pallas kernels, barotropic_steps(): pl.pallas_call(step_kernel, out_shape=(f32(4, ROWS, COLS), f32(ROWS, COLS...  6.74 us
  transfers between devices with their start and end apart: 14, of which 6 were waited for; matrix products, arithmetic and copies ran while one was open for 0% of the time, Pallas kernels for 16%

commit v1 on v0

--- a/solution.py
+++ b/solution.py
@@ -146,7 +146,14 @@
 
     def put(d, where=y_ref):
         to = d if slots == 1 else (lon + d) % seats
-        return pltpu.make_async_copy(where.at[d], y_hbm.at[to], out_sem.at[d])
+        return pltpu.make_async_copy(where.at[d], y_hbm.at[to], out_sem.at[d, 0])
+
+    spans = ((0, 56), (176, 104), (400, 50), (56, 120), (280, 120))
+
+    def put_rows(d, j):
+        to = d if slots == 1 else (lon + d) % seats
+        at = pl.ds(*spans[j])
+        return pltpu.make_async_copy(y_ref.at[d, at], y_hbm.at[to, at], out_sem.at[d, j])
 
     two = 2 * lanes
 
@@ -255,6 +262,10 @@
             for s in range(16):
                 y_ref[s // 2, pl.ds(s % 2 * SEG, 1), lane] = ys[s]
             for i in range(HALF // 8):
+                if i == HALF // 16:
+                    for d in range(seats):
+                        for j in (0, 1, 2):
+                            put_rows(d, j).start()
                 rows = pl.ds(8 * i, 8)
                 tw = tw_ref[rows, :]
                 re_at, im_at = spots(g, 0)
@@ -273,9 +284,11 @@
         for g in range(lanes // 128):
             inverse(g)
         for d in range(seats):
-            put(d).start()
+            for j in (3, 4):
+                put_rows(d, j).start()
         for d in range(seats):
-            put(d).wait()
+            for j in range(5):
+                put_rows(d, j).wait()
 
 
 def filter_call(xs, cut, tables, twist, shape):
@@ -283,7 +296,7 @@
     seats = shape[0]
     vmem = pl.BlockSpec(memory_space=pltpu.VMEM)
     far = pl.BlockSpec(memory_space=pltpu.HBM)
-    dma = pltpu.SemaphoreType.DMA((seats,))
+    dma = pltpu.SemaphoreType.DMA((seats, 5))
     operands = (*xs, cut, *tables, twist)
     return pl.pallas_call(
         functools.partial(filter_kernel, slots=len(xs)),

time: 151 us -> 151 us (level)
  no operation moved by 1% of the time
where the time goes in v1:
time: 151 us; the launch traced here: 150 us
  starting transfers between devices  59.1 us (39%)
  waiting for transfers between devices  58.2 us (39%)
  Pallas kernels  29.3 us (19%)
  local copies, waits for them, and re-layouts  1.96 us (1%)
    ppermute x7, starting transfers between devices, body(): got.append(lax.ppermute(slots[k], ('lon', 'lat'), route))  31.9 us
    ppermute x4, waiting for transfers between devices, shift(): lax.ppermute(value, axis, [(i, (i + by) % size) for i in range(size)])  24.2 us
    all_to_all x1, waiting for transfers between devices, body(): got = lax.all_to_all(got, 'lon', split_axis=0, concat_axis=0)  20.1 us
    ppermute x7, waiting for transfers between devices, body(): got.append(lax.ppermute(slots[k], ('lon', 'lat'), route))  14 us
    all_to_all x2, starting transfers between devices, body(): parts = lax.all_to_all(parts, 'lon', split_axis=0, concat_axis=0)  11.7 us
    pallas_call x2, Pallas kernels, filter_call(): pl.pallas_call(functools.partial(filter_kernel, slots=len(xs)), out_shape...  11.5 us
    ppermute x4, starting transfers between devices, shift(): lax.ppermute(value, axis, [(i, (i + by) % size) for i in range(size)])  9.55 us
    pallas_call x1, Pallas kernels, barotropic_steps(): pl.pallas_call(step_kernel, out_shape=(f32(4, ROWS, COLS), f32(ROWS, COLS...  6.74 us
  transfers between devices with their start and end apart: 14, of which 6 were waited for; matrix products, arithmetic and copies ran while one was open for 0% of the time, Pallas kernels for 16%

profile of v1, /device:TPU:0, one launch (start us, length us, event | category | flops | bytes accessed | tf_op | source)
XLA Modules:
  0.0 149.5 jit_solution(15107116313584820241)
XLA Ops:
  0.6 3.5 %pack_flow.1 = f32[8,450,128]{2,1,0:T(8,128)} custom-call(f32[8]{0:T(128)} %thick_ref.1, f32[32,64,450]{2,1,0:T(8,128)} %bitcast.4), custom_call_target="tpu_custom_call" | custom-call | tf_op jit(solution)/shard_map/pack_flow/pallas_call | solution.py:592
  4.1 8.1 %all-to-all-start.1 = ((f32[8,450,128]{2,1,0:T(8,128)}), f32[8,450,128]{2,1,0:T(8,128)S(1)}, u32[]{:S(2)}, u32[]{:S(2)}) async-start(f32[8,450,128]{2,1,0:T(8,128)} %pack_flow.1), calls=%async_computation.1 | async-start | bytes 3735552 | tf_op jit(solution)/shard_map/all_to_all | solution.py:606
  12.2 2.9 %pack_tracers.1 = (f32[450,128]{1,0:T(8,128)}, f32[450,128]{1,0:T(8,128)}, f32[450,128]{1,0:T(8,128)}, f32[450,128]{1,0:T(8,128)}, f32[450,128]{1,0:T(8,128)}, /...) custom-call(f32[32,64,450]{2,1,0:T(8,128)} %bitcast.5), custom_call_target="tpu_custom_call" | custom-call | tf_op jit(solution)/shard_map/pack_tracers/pallas_call | solution.py:607
  15.2 7.5 %collective-permute-start = (f32[450,128]{1,0:T(8,128)}, f32[450,128]{1,0:T(8,128)S(1)}, u32[]{:S(2)}, u32[]{:S(2)}) collective-permute-start(f32[450,128]{1,0:T(8,128)} %get-tuple-element.19), channel_id=1, source_target_pairs={{0,112},{16,0},{32,16},{48,32},{64,48},{80,64},{96,80},{112,96},{1... | collective-permute-start | bytes 691208 | tf_op jit(solution)/shard_map/ppermute | solution.py:626
  22.7 2.8 %collective-permute-start.1 = (f32[450,128]{1,0:T(8,128)}, f32[450,128]{1,0:T(8,128)S(1)}, u32[]{:S(2)}, u32[]{:S(2)}) collective-permute-start(f32[450,128]{1,0:T(8,128)} %get-tuple-element.20), channel_id=1, source_target_pairs={{0,96},{16,112},{32,0},{48,16},{64,32},{80,48},{96,64},{112,80},{1... | collective-permute-start | bytes 691208 | tf_op jit(solution)/shard_map/ppermute | solution.py:626
  25.5 2.5 %collective-permute-start.2 = (f32[450,128]{1,0:T(8,128)}, f32[450,128]{1,0:T(8,128)S(1)}, u32[]{:S(2)}, u32[]{:S(2)}) collective-permute-start(f32[450,128]{1,0:T(8,128)} %get-tuple-element.21), channel_id=1, source_target_pairs={{0,80},{16,96},{32,112},{48,0},{64,16},{80,32},{96,48},{112,64},{1... | collective-permute-start | bytes 691208 | tf_op jit(solution)/shard_map/ppermute | solution.py:626
  27.9 4.6 %collective-permute-start.3 = (f32[450,128]{1,0:T(8,128)}, f32[450,128]{1,0:T(8,128)S(1)}, u32[]{:S(2)}, u32[]{:S(2)}) collective-permute-start(f32[450,128]{1,0:T(8,128)} %get-tuple-element.22), channel_id=1, source_target_pairs={{0,64},{16,80},{32,96},{48,112},{64,0},{80,16},{96,32},{112,48},{1... | collective-permute-start | bytes 691208 | tf_op jit(solution)/shard_map/ppermute | solution.py:626
  32.5 3.1 %collective-permute-start.4 = (f32[450,128]{1,0:T(8,128)}, f32[450,128]{1,0:T(8,128)S(1)}, u32[]{:S(2)}, u32[]{:S(2)}) collective-permute-start(f32[450,128]{1,0:T(8,128)} %get-tuple-element.23), channel_id=1, source_target_pairs={{0,48},{16,64},{32,80},{48,96},{64,112},{80,0},{96,16},{112,32},{1... | collective-permute-start | bytes 691208 | tf_op jit(solution)/shard_map/ppermute | solution.py:626
  35.7 7.4 %collective-permute-done.refs_1_ = f32[450,128]{1,0:T(8,128)S(1)} collective-permute-done((f32[450,128]{1,0:T(8,128)}, f32[450,128]{1,0:T(8,128)S(1)}, u32[]{:S(2)}, u32[]{:S(2)}) %collective-permute-start) | collective-permute-done | bytes 230432 | tf_op jit(solution)/shard_map/ppermute | solution.py:626
  43.1 2.8 %collective-permute-start.5 = (f32[450,128]{1,0:T(8,128)}, f32[450,128]{1,0:T(8,128)S(1)}, u32[]{:S(2)}, u32[]{:S(2)}) collective-permute-start(f32[450,128]{1,0:T(8,128)} %get-tuple-element.24), channel_id=1, source_target_pairs={{0,32},{16,48},{32,64},{48,80},{64,96},{80,112},{96,0},{112,16},{1... | collective-permute-start | bytes 691208 | tf_op jit(solution)/shard_map/ppermute | solution.py:626
  45.9 8.6 %collective-permute-start.6 = (f32[450,128]{1,0:T(8,128)}, f32[450,128]{1,0:T(8,128)}, u32[]{:S(2)}, u32[]{:S(2)}) collective-permute-start(f32[450,128]{1,0:T(8,128)} %get-tuple-element.25), channel_id=1, source_target_pairs={{0,16},{16,32},{32,48},{48,64},{64,80},{80,96},{96,112},{112,0},{1... | collective-permute-start | bytes 691208 | tf_op jit(solution)/shard_map/ppermute | solution.py:626
  54.7 6.5 %collective-permute-done.5.refs_6_ = f32[450,128]{1,0:T(8,128)S(1)} collective-permute-done((f32[450,128]{1,0:T(8,128)}, f32[450,128]{1,0:T(8,128)S(1)}, u32[]{:S(2)}, u32[]{:S(2)}) %collective-permute-start.5) | collective-permute-done | bytes 230432 | tf_op jit(solution)/shard_map/ppermute | solution.py:626
  63.0 6.2 %polar_filter.2 = f32[8,450,128]{2,1,0:T(8,128)} custom-call(f32[450,128]{1,0:T(8,128)S(1)} %copy-done.4, f32[450,128]{1,0:T(8,128)S(1)} %collective-permute-done.refs_1_, f32[450,128]{1,0:T(8,128)S(1)} %collective-permute-done.1.refs_2_, f32[450,128]{1,0:T(8,128)S(1)} %collective-permute-done.2.refs_3_, f32[450,128]{1,0:T(8,128)S(1)} %collective-permute-done.3.refs_4_, ...), custom_call_target="tpu_custom_call" | custom-call | tf_op jit(solution)/shard_map/polar_filter/pallas_call | solution.py:301
  69.3 6.0 %all-to-all-start = ((f32[8,450,128]{2,1,0:T(8,128)}), f32[8,450,128]{2,1,0:T(8,128)}, u32[]{:S(2)}, u32[]{:S(2)}) async-start(f32[8,450,128]{2,1,0:T(8,128)} %polar_filter.2), calls=%async_computation | async-start | bytes 3735552 | tf_op jit(solution)/shard_map/all_to_all | solution.py:632
  75.3 5.3 %polar_filter.3 = f32[8,450,128]{2,1,0:T(8,128)} custom-call(f32[8,450,128]{2,1,0:T(8,128)S(1)} %all-to-all-done.1.refs_0_, s32[1,128]{1,0:T(1,128)S(1)} %broadcast_in_dim_tile.3.refs_8_.refs_1_, bf16[2,128,256]{2,1,0:T(8,128)(2,1)S(1)} %copy-done.2, bf16[2,128,256]{2,1,0:T(8,128)(2,1)S(1)} %copy-done.1, f32[112,16]{1,0:T(8,128)S(1)} %copy-done.6), custom_call_target="tpu_custom_call" | custom-call | tf_op jit(solution)/shard_map/polar_filter/pallas_call | solution.py:301
  80.6 20.1 %all-to-all-done.got_hbm = f32[8,450,128]{2,1,0:T(8,128)} async-done(((f32[8,450,128]{2,1,0:T(8,128)}), f32[8,450,128]{2,1,0:T(8,128)}, u32[]{:S(2)}, u32[]{:S(2)}) %all-to-all-start) | async-done | bytes 1843232 | tf_op jit(solution)/shard_map/all_to_all | solution.py:632
  100.7 3.6 %all-to-all-start.2 = ((f32[8,450,128]{2,1,0:T(8,128)}), f32[8,450,128]{2,1,0:T(8,128)S(1)}, u32[]{:S(2)}, u32[]{:S(2)}) async-start(f32[8,450,128]{2,1,0:T(8,128)} %polar_filter.3), calls=%async_computation.2 | async-start | bytes 3735552 | tf_op jit(solution)/shard_map/all_to_all | solution.py:629
  104.4 5.6 %collective-permute-start.7 = (f32[64,128]{1,0:T(8,128)S(1)}, f32[64,128]{1,0:T(8,128)S(1)}, u32[]{:S(2)}, u32[]{:S(2)}) collective-permute-start(f32[64,128]{1,0:T(8,128)S(1)} %get-tuple-element.26), channel_id=1, source_target_pairs={{0,112},{16,0},{32,16},{48,32},{64,48},{80,64},{96,80},{112,96},{1... | collective-permute-start | bytes 98312 | tf_op jit(solution)/shard_map/ppermute | solution.py:568
  110.1 18.4 %collective-permute-done.7.east_ref = f32[64,128]{1,0:T(8,128)S(1)} collective-permute-done((f32[64,128]{1,0:T(8,128)S(1)}, f32[64,128]{1,0:T(8,128)S(1)}, u32[]{:S(2)}, u32[]{:S(2)}) %collective-permute-start.7) | collective-permute-done | bytes 32800 | tf_op jit(solution)/shard_map/ppermute | solution.py:568
  128.5 2.5 %collective-permute-done.8.west_ref = f32[64,128]{1,0:T(8,128)S(1)} collective-permute-done((f32[64,128]{1,0:T(8,128)S(1)}, f32[64,128]{1,0:T(8,128)S(1)}, u32[]{:S(2)}, u32[]{:S(2)}) %collective-permute-start.8) | collective-permute-done | bytes 32800 | tf_op jit(solution)/shard_map/ppermute | solution.py:568
  131.2 3.8 %collective-permute-start.10 = (f32[4,24,512]{2,1,0:T(8,128)S(1)}, f32[4,24,512]{2,1,0:T(8,128)S(1)}, u32[]{:S(2)}, u32[]{:S(2)}) collective-permute-start(f32[4,24,512]{2,1,0:T(8,128)S(1)} %get-tuple-element.30), channel_id=1, source_target_pairs={{0,15},{1,0},{2,1},{3,2},{4,3},{5,4},{6,5},{7,6},{8,7},{9,8},{10,9... | collective-permute-start | bytes 589832 | tf_op jit(solution)/shard_map/ppermute | solution.py:568
  135.1 3.3 %collective-permute-done.9.top_ref = f32[4,24,512]{2,1,0:T(8,128)S(1)} collective-permute-done((f32[4,24,512]{2,1,0:T(8,128)S(1)}, f32[4,24,512]{2,1,0:T(8,128)S(1)}, u32[]{:S(2)}, u32[]{:S(2)}) %collective-permute-start.9) | collective-permute-done | bytes 196640 | tf_op jit(solution)/shard_map/ppermute | solution.py:568
  138.4 6.7 %subcycles.1 = (f32[4,64,450]{2,1,0:T(8,128)S(1)}, f32[64,450]{1,0:T(8,128)}) custom-call(s32[2]{0:T(128)S(1)} %pad_add_fusion.at_ref, f32[4,64,512]{2,1,0:T(8,128)S(1)} %get-tuple-element.28.mid_ref, f32[4,24,512]{2,1,0:T(8,128)S(1)} %collective-permute-done.9.top_ref, f32[4,24,512]{2,1,0:T(8,128)S(1)} %collective-permute-done.10.low_ref), custom_call_target="tpu_custom_call" | custom-call | tf_op jit(solution)/shard_map/subcycles/pallas_call | solution.py:449
  145.1 2.9 %unpack_tracers.1 = f32[16,64,450]{2,1,0:T(8,128)} custom-call(f32[8,450,128]{2,1,0:T(8,128)} %all-to-all-done.got_hbm, f32[32,64,450]{2,1,0:T(8,128)} %bitcast.6), custom_call_target="tpu_custom_call" | custom-call | tf_op jit(solution)/shard_map/unpack_tracers/pallas_call | solution.py:645
  (33 shorter events, 3.9 us)
Async XLA Ops:
  4.1 65.2 %all-to-all-start.1 = ((f32[8,450,128]{2,1,0:T(8,128)}), f32[8,450,128]{2,1,0:T(8,128)S(1)}, u32[]{:S(2)}, u32[]{:S(2)}) async-start(f32[8,450,128]{2,1,0:T(8,128)} %pack_flow.1), calls=%async_computation.1 | async-start | bytes 3735552 | tf_op jit(solution)/shard_map/all_to_all | solution.py:606
  12.2 42.4 %copy-start.7 = (s32[256]{0:T(256)S(1)}, s32[256]{0:T(256)}, u32[]{:S(2)}) copy-start(s32[256]{0:T(256)} %param.9) | copy-start | bytes 3076
  12.2 49.1 %copy-start.1 = (bf16[2,128,256]{2,1,0:T(8,128)(2,1)S(1)}, bf16[2,128,256]{2,1,0:T(8,128)(2,1)}, u32[]{:S(2)}) copy-start(bf16[2,128,256]{2,1,0:T(8,128)(2,1)} %constant.31.refs_10_.refs_3_) | copy-start | bytes 393220
  12.2 49.0 %copy-start.2 = (bf16[2,128,256]{2,1,0:T(8,128)(2,1)S(1)}, bf16[2,128,256]{2,1,0:T(8,128)(2,1)}, u32[]{:S(2)}) copy-start(bf16[2,128,256]{2,1,0:T(8,128)(2,1)} %constant.28.refs_9_.refs_2_) | copy-start | bytes 393220
  15.2 27.9 %collective-permute-start = (f32[450,128]{1,0:T(8,128)}, f32[450,128]{1,0:T(8,128)S(1)}, u32[]{:S(2)}, u32[]{:S(2)}) collective-permute-start(f32[450,128]{1,0:T(8,128)} %get-tuple-element.19), channel_id=1, source_target_pairs={{0,112},{16,0},{32,16},{48,32},{64,48},{80,64},{96,80},{112,96},{1... | collective-permute-start | bytes 691208 | tf_op jit(solution)/shard_map/ppermute | solution.py:626
  22.7 23.2 %collective-permute-start.1 = (f32[450,128]{1,0:T(8,128)}, f32[450,128]{1,0:T(8,128)S(1)}, u32[]{:S(2)}, u32[]{:S(2)}) collective-permute-start(f32[450,128]{1,0:T(8,128)} %get-tuple-element.20), channel_id=1, source_target_pairs={{0,96},{16,112},{32,0},{48,16},{64,32},{80,48},{96,64},{112,80},{1... | collective-permute-start | bytes 691208 | tf_op jit(solution)/shard_map/ppermute | solution.py:626
  25.5 29.3 %collective-permute-start.2 = (f32[450,128]{1,0:T(8,128)}, f32[450,128]{1,0:T(8,128)S(1)}, u32[]{:S(2)}, u32[]{:S(2)}) collective-permute-start(f32[450,128]{1,0:T(8,128)} %get-tuple-element.21), channel_id=1, source_target_pairs={{0,80},{16,96},{32,112},{48,0},{64,16},{80,32},{96,48},{112,64},{1... | collective-permute-start | bytes 691208 | tf_op jit(solution)/shard_map/ppermute | solution.py:626
  27.9 26.8 %collective-permute-start.3 = (f32[450,128]{1,0:T(8,128)}, f32[450,128]{1,0:T(8,128)S(1)}, u32[]{:S(2)}, u32[]{:S(2)}) collective-permute-start(f32[450,128]{1,0:T(8,128)} %get-tuple-element.22), channel_id=1, source_target_pairs={{0,64},{16,80},{32,96},{48,112},{64,0},{80,16},{96,32},{112,48},{1... | collective-permute-start | bytes 691208 | tf_op jit(solution)/shard_map/ppermute | solution.py:626
  32.5 22.2 %collective-permute-start.4 = (f32[450,128]{1,0:T(8,128)}, f32[450,128]{1,0:T(8,128)S(1)}, u32[]{:S(2)}, u32[]{:S(2)}) collective-permute-start(f32[450,128]{1,0:T(8,128)} %get-tuple-element.23), channel_id=1, source_target_pairs={{0,48},{16,64},{32,80},{48,96},{64,112},{80,0},{96,16},{112,32},{1... | collective-permute-start | bytes 691208 | tf_op jit(solution)/shard_map/ppermute | solution.py:626
  43.1 18.2 %collective-permute-start.5 = (f32[450,128]{1,0:T(8,128)}, f32[450,128]{1,0:T(8,128)S(1)}, u32[]{:S(2)}, u32[]{:S(2)}) collective-permute-start(f32[450,128]{1,0:T(8,128)} %get-tuple-element.24), channel_id=1, source_target_pairs={{0,32},{16,48},{32,64},{48,80},{64,96},{80,112},{96,0},{112,16},{1... | collective-permute-start | bytes 691208 | tf_op jit(solution)/shard_map/ppermute | solution.py:626
  45.9 15.4 %collective-permute-start.6 = (f32[450,128]{1,0:T(8,128)}, f32[450,128]{1,0:T(8,128)}, u32[]{:S(2)}, u32[]{:S(2)}) collective-permute-start(f32[450,128]{1,0:T(8,128)} %get-tuple-element.25), channel_id=1, source_target_pairs={{0,16},{16,32},{32,48},{48,64},{64,80},{80,96},{96,112},{112,0},{1... | collective-permute-start | bytes 691208 | tf_op jit(solution)/shard_map/ppermute | solution.py:626
  61.3 0.9 copy-start.4
  62.2 0.8 copy-start.5
  69.3 6.0 %copy-start.6 = (f32[112,16]{1,0:T(8,128)S(1)}, f32[112,16]{1,0:T(8,128)}, u32[]{:S(2)}) copy-start(f32[112,16]{1,0:T(8,128)} %constant.24.clone.refs_11_.refs_4_) | copy-start | bytes 21508
  69.3 31.4 %all-to-all-start = ((f32[8,450,128]{2,1,0:T(8,128)}), f32[8,450,128]{2,1,0:T(8,128)}, u32[]{:S(2)}, u32[]{:S(2)}) async-start(f32[8,450,128]{2,1,0:T(8,128)} %polar_filter.2), calls=%async_computation | async-start | bytes 3735552 | tf_op jit(solution)/shard_map/all_to_all | solution.py:632
  80.6 23.7 %copy-start = (f32[3,64,450]{2,1,0:T(8,128)S(1)}, f32[3,64,450]{2,1,0:T(8,128)}, u32[]{:S(2)}) copy-start(f32[3,64,450]{2,1,0:T(8,128)} %flow_ref.3) | copy-start | bytes 1036804
  80.6 23.7 %copy-start.3 = (s32[64,450]{1,0:T(8,128)S(1)}, s32[64,450]{1,0:T(8,128)}, u32[]{:S(2)}) copy-start(s32[64,450]{1,0:T(8,128)} %land_ref.3) | copy-start | bytes 345604
  100.7 47.3 %all-to-all-start.2 = ((f32[8,450,128]{2,1,0:T(8,128)}), f32[8,450,128]{2,1,0:T(8,128)S(1)}, u32[]{:S(2)}, u32[]{:S(2)}) async-start(f32[8,450,128]{2,1,0:T(8,128)} %polar_filter.3), calls=%async_computation.2 | async-start | bytes 3735552 | tf_op jit(solution)/shard_map/all_to_all | solution.py:629
  104.4 24.0 %collective-permute-start.7 = (f32[64,128]{1,0:T(8,128)S(1)}, f32[64,128]{1,0:T(8,128)S(1)}, u32[]{:S(2)}, u32[]{:S(2)}) collective-permute-start(f32[64,128]{1,0:T(8,128)S(1)} %get-tuple-element.26), channel_id=1, source_target_pairs={{0,112},{16,0},{32,16},{48,32},{64,48},{80,64},{96,80},{112,96},{1... | collective-permute-start | bytes 98312 | tf_op jit(solution)/shard_map/ppermute | solution.py:568
  110.1 20.9 %collective-permute-start.8 = (f32[64,128]{1,0:T(8,128)S(1)}, f32[64,128]{1,0:T(8,128)S(1)}, u32[]{:S(2)}, u32[]{:S(2)}) collective-permute-start(f32[64,128]{1,0:T(8,128)S(1)} %get-tuple-element.27), channel_id=1, source_target_pairs={{0,16},{16,32},{32,48},{48,64},{64,80},{80,96},{96,112},{112,0},{1... | collective-permute-start | bytes 98312 | tf_op jit(solution)/shard_map/ppermute | solution.py:568
  131.1 7.3 %collective-permute-start.9 = (f32[4,24,512]{2,1,0:T(8,128)S(1)}, f32[4,24,512]{2,1,0:T(8,128)S(1)}, u32[]{:S(2)}, u32[]{:S(2)}) collective-permute-start(f32[4,24,512]{2,1,0:T(8,128)S(1)} %get-tuple-element.29), channel_id=1, source_target_pairs={{0,1},{1,2},{2,3},{3,4},{4,5},{5,6},{6,7},{7,8},{8,9},{9,10},{10,1... | collective-permute-start | bytes 589832 | tf_op jit(solution)/shard_map/ppermute | solution.py:568
  131.2 7.2 %collective-permute-start.10 = (f32[4,24,512]{2,1,0:T(8,128)S(1)}, f32[4,24,512]{2,1,0:T(8,128)S(1)}, u32[]{:S(2)}, u32[]{:S(2)}) collective-permute-start(f32[4,24,512]{2,1,0:T(8,128)S(1)} %get-tuple-element.30), channel_id=1, source_target_pairs={{0,15},{1,0},{2,1},{3,2},{4,3},{5,4},{6,5},{7,6},{8,7},{9,8},{10,9... | collective-permute-start | bytes 589832 | tf_op jit(solution)/shard_map/ppermute | solution.py:568
